TPU v7x, 256 devices: a whole 4x4x8 slice. The times are simulated.
256 devices in a mesh: pp: 4 (over x_hi, core), tp: 16 (over z, x_lo), dp: 4 (over y).
Axes of the slice: x: 4 (x_hi: 2, x_lo: 2; x = x_hi * 2 + x_lo), y: 4, z: 8, core: 2. Of those that a mesh axis runs over, the one named last changes fastest.
Arguments:
- layer_input: bfloat16 [4, 4, 128, 4096], P('pp', 'dp', 'tp'), may hold values from -4 to 4
- gate_pre: bfloat16 [4, 4, 128, 14784], P('pp', 'dp', None, 'tp'), may hold values from -8 to 8
- up_pre: bfloat16 [4, 4, 128, 14784], P('pp', 'dp', None, 'tp'), may hold values from -6 to 6
- hidden_grad: bfloat16 [4, 4, 128, 14784], P('pp', 'dp', None, 'tp'), may hold values from -0.59765625 to 0.59765625
- gate_weight: bfloat16 [4, 4096, 14784], P('pp', 'dp', 'tp'), may hold values from -0.09375 to 0.09375
Outputs:
- passed_grad: bfloat16 [4, 4, 128, 4096], P('pp', 'dp', 'tp')
- gate_weight_grad: bfloat16 [4, 4096, 14784], P('pp', 'dp', 'tp')
All inputs are finite; a program needn't handle non-finite values.
Results may differ from a plain program's by a relative error of at most 0.018.
Values may be sent and summed in bfloat16 or wider, within the bound.
A program may use at most 64 MiB of HBM per device.

v0:
```python
import jax
import jax.numpy as jnp
from jax import lax
from jax.sharding import PartitionSpec as P


def cut_along(x, dim, peers):
    before, after = (x.shape[:dim], x.shape[dim + 1 :])
    return jnp.moveaxis(x.reshape(*before, peers, -1, *after), dim, 0)


def sent_and_summed(x, axis, dim):
    tiles = cut_along(x, dim, lax.axis_size(axis))
    arrived = lax.all_to_all(tiles, axis, split_axis=0, concat_axis=0, tiled=True)
    return arrived.astype(jnp.float32).sum(axis=0)


def from_everyone(x, axis):
    copies = jnp.broadcast_to(x, (lax.axis_size(axis), *x.shape))
    return lax.all_to_all(copies, axis, split_axis=0, concat_axis=0, tiled=True)


def laid_out(tiles, dim):
    tiles = jnp.moveaxis(tiles, 0, dim)
    lengths = tiles.shape
    return tiles.reshape(*lengths[:dim], lengths[dim] * lengths[dim + 1], *lengths[dim + 2 :])


def collect(x, axis, dim):
    tiles = from_everyone(x, axis)
    return laid_out(tiles, dim)


def from_behind(block, axis, distance):
    devices = range(lax.axis_size(axis))
    route = [(i - distance, i) for i in devices if i - distance in devices]
    return lax.ppermute(block, axis, route)


def finish(partial_value):
    return sent_and_summed(partial_value.astype(jnp.bfloat16), "tp", 0).astype(jnp.bfloat16)


def on_device(layer_input, gate_pre, up_pre, hidden_grad, gate_weight):
    tokens_in = layer_input[0, 0]
    gate_val = gate_pre[0, 0].astype(jnp.float32)
    up_val = up_pre[0, 0].astype(jnp.float32)
    hidden_val = hidden_grad[0, 0].astype(jnp.float32)
    gate_local = gate_weight[0]
    rows_total = gate_val.shape[0]
    groups = lax.axis_size("dp")
    logistic = jax.nn.sigmoid(gate_val)
    gate_grad = (hidden_val * up_val * logistic * (1.0 + gate_val * (1.0 - logistic))).astype(
        jnp.bfloat16
    )
    gathered_in = collect(tokens_in, "tp", 0)
    contract_cols = (((1,), (1,)), ((), ()))
    all_grads = collect(gate_grad, "dp", 0)
    partial_value = lax.dot_general(
        all_grads, gate_local, contract_cols, preferred_element_type=jnp.float32
    )
    returned = lax.all_to_all(
        partial_value.astype(jnp.bfloat16), "dp", split_axis=0, concat_axis=1, tiled=True
    ).astype(partial_value.dtype)
    input_grad = finish(returned)
    in_columns = lax.all_to_all(gathered_in, "dp", split_axis=1, concat_axis=0, tiled=True)
    products = lax.dot_general(
        in_columns.reshape(groups, rows_total, in_columns.shape[1]),
        all_grads.reshape(groups, rows_total, all_grads.shape[1]),
        (((1,), (1,)), ((0,), (0,))),
        preferred_element_type=jnp.float32,
    )
    rounded = lax.optimization_barrier(products.astype(jnp.bfloat16))
    grads_total = jnp.sum(rounded.astype(jnp.float32), axis=0)
    passed = from_behind(input_grad, "pp", -1)
    gate_out = grads_total.astype(jnp.bfloat16)
    return (passed[None, None], gate_out[None])


def solution(mesh):
    return jax.shard_map(
        on_device,
        mesh=mesh,
        in_specs=(
            P("pp", "dp", "tp", None),
            P("pp", "dp", None, "tp"),
            P("pp", "dp", None, "tp"),
            P("pp", "dp", None, "tp"),
            P("pp", "dp", "tp"),
        ),
        out_specs=(P("pp", "dp", "tp", None), P("pp", "dp", "tp")),
        check_vma=False,
    )
```

profile of v0, /device:TPU:96, one launch (start us, length us, event | category | flops | bytes accessed | tf_op | source)
XLA Modules:
  0.0 136.5 jit_solution(6257464139573123061)
XLA Ops:
  0.6 1.5 %fusion.11 = bf16[128,924]{0,1:T(8,128)(2,1)S(1)} fusion(bf16[1,1,128,924]{2,3,1,0:T(8,128)(2,1)} %param.7, bf16[1,1,128,924]{2,3,1,0:T(8,128)(2,1)} %param.8, bf16[1,1,128,924]{2,3,1,0:T(8,128)(2,1)} %param.6), kind=kLoop, calls=%fused_computation.13 | loop fusion | flops 1537536 | bytes 946176 | tf_op jit(solution)/shard_map/convert_element_type | solution.py:53
  2.2 0.1 broadcast_in_dim.12
  2.3 18.3 %all_to_all.47 = bf16[4,128,924]{1,2,0:T(8,128)(2,1)S(1)} all-to-all(bf16[4,128,924]{1,2,0:T(8,128)(2,1)S(1)} %broadcast_in_dim.12), channel_id=1, replica_groups=mesh['pp'=4,'tp'=16,'dp'=4] {'dp'}, dimensions={0} | all-to-all | bytes 1892352 | tf_op jit(solution)/shard_map/all_to_all | solution.py:20
  20.6 0.5 copy.15
  21.1 0.4 pad
  21.5 0.2 copy.13
  21.7 1.3 fusion.2
  23.0 17.2 %all_to_all.48 = bf16[4,128,1024]{2,1,0:T(8,128)(2,1)} all-to-all(bf16[4,128,1024]{2,1,0:T(8,128)(2,1)S(1)} %bitcast.35), channel_id=1, replica_groups=mesh['pp'=4,'tp'=16,'dp'=4] {'dp'}, dimensions={0} | all-to-all | bytes 2097152 | tf_op jit(solution)/shard_map/all_to_all | solution.py:62
  40.2 1.1 broadcast_in_dim.14
  41.3 8.6 %all-to-all-start.3 = ((bf16[16,8,4096]{2,1,0:T(8,128)(2,1)}), bf16[16,8,4096]{2,1,0:T(8,128)(2,1)}, u32[]{:S(2)}, u32[]{:S(2)}) async-start(bf16[16,8,4096]{2,1,0:T(8,128)(2,1)} %broadcast_in_dim.14), calls=%async_computation.3 | async-start | bytes 2097152 | tf_op jit(solution)/shard_map/all_to_all | solution.py:20
  49.9 3.0 %copy.11 = bf16[128,4,1024]{2,1,0:T(4,128)(2,1)} copy(bf16[128,4,1024]{2,0,1:T(8,128)(2,1)} %bitcast.31) | data formatting | bytes 2097152 | tf_op jit(solution)/shard_map/all_to_all | solution.py:62
  52.9 2.6 %reshape.27 = bf16[16,8,4096]{2,1,0:T(8,128)(2,1)} reshape(bf16[128,4,1024]{2,1,0:T(4,128)(2,1)} %copy.11) | data formatting | bytes 2097152 | tf_op jit(solution)/shard_map/reshape | solution.py:9
  55.5 18.3 %all-to-all-done.3 = bf16[16,8,4096]{2,1,0:T(8,128)(2,1)} async-done(((bf16[16,8,4096]{2,1,0:T(8,128)(2,1)}), bf16[16,8,4096]{2,1,0:T(8,128)(2,1)}, u32[]{:S(2)}, u32[]{:S(2)}) %all-to-all-start.3) | async-done | bytes 1048608 | tf_op jit(solution)/shard_map/all_to_all | solution.py:20
  73.8 6.0 %all-to-all-start.2 = ((bf16[16,8,4096]{2,1,0:T(8,128)(2,1)}), bf16[16,8,4096]{2,1,0:T(8,128)(2,1)}, u32[]{:S(2)}, u32[]{:S(2)}) async-start(bf16[16,8,4096]{2,1,0:T(8,128)(2,1)} %reshape.27), calls=%async_computation.2 | async-start | bytes 2097152 | tf_op jit(solution)/shard_map/all_to_all | solution.py:14
  79.8 2.6 %all_to_all.39 = bf16[128,4,1024]{2,1,0:T(4,128)(2,1)} reshape(bf16[16,8,4096]{2,1,0:T(8,128)(2,1)} %all-to-all-done.3) | data formatting | bytes 2097152 | tf_op jit(solution)/shard_map/all_to_all | solution.py:66
  82.4 2.6 %copy.12 = bf16[128,4,1024]{2,0,1:T(8,128)(2,1)} copy(bf16[128,4,1024]{2,1,0:T(4,128)(2,1)} %all_to_all.39) | data formatting | bytes 2097152 | tf_op jit(solution)/shard_map/all_to_all | solution.py:66
  85.0 19.1 %all-to-all-done.2 = bf16[16,8,4096]{2,1,0:T(8,128)(2,1)} async-done(((bf16[16,8,4096]{2,1,0:T(8,128)(2,1)}), bf16[16,8,4096]{2,1,0:T(8,128)(2,1)}, u32[]{:S(2)}, u32[]{:S(2)}) %all-to-all-start.2) | async-done | bytes 1048608 | tf_op jit(solution)/shard_map/all_to_all | solution.py:14
  104.1 4.2 %all-to-all-start.4 = ((bf16[128,4,1024]{2,0,1:T(8,128)(2,1)}), bf16[128,4,1024]{2,0,1:T(8,128)(2,1)}, u32[]{:S(2)}, u32[]{:S(2)}) async-start(bf16[128,4,1024]{2,0,1:T(8,128)(2,1)} %copy.12), calls=%async_computation.4 | async-start | bytes 2097152 | tf_op jit(solution)/shard_map/all_to_all | solution.py:66
  108.3 1.4 %reduce_sum.24 = bf16[8,4096]{1,0:T(8,128)(2,1)S(1)} reduce(bf16[16,8,4096]{2,1,0:T(8,128)(2,1)} %all-to-all-done.2, bf16[]{:T(256)} %constant.5.clone.1), dimensions={0}, to_apply=%region_0.0 | reduce | flops 491520 | bytes 1114114 | tf_op jit(solution)/shard_map/reduce_sum | solution.py:15
  109.7 1.3 collective-permute-start
  111.0 11.7 %all-to-all-done.4 = bf16[128,4,1024]{2,0,1:T(8,128)(2,1)} async-done(((bf16[128,4,1024]{2,0,1:T(8,128)(2,1)}), bf16[128,4,1024]{2,0,1:T(8,128)(2,1)}, u32[]{:S(2)}, u32[]{:S(2)}) %all-to-all-start.4) | async-done | bytes 1048608 | tf_op jit(solution)/shard_map/all_to_all | solution.py:66
  122.6 6.4 %convert_bitcast_fusion = bf16[4,1024,924]{1,2,0:T(8,128)(2,1)} fusion(bf16[4,128,924]{1,2,0:T(8,128)(2,1)S(1)} %all_to_all.47, bf16[128,4,1024]{2,0,1:T(8,128)(2,1)} %all-to-all-done.4), kind=kOutput, calls=%fused_computation | convolution fusion | flops 972668928 | bytes 9564160 | tf_op jit(solution)/shard_map/dot_general | solution.py:67
  129.0 6.9 %reduce_sum.25 = bf16[1024,924]{0,1:T(8,128)(2,1)} reduce(bf16[4,1024,924]{1,2,0:T(8,128)(2,1)} %convert_bitcast_fusion, bf16[]{:T(256)} %constant.5.clone.1), dimensions={0}, to_apply=%region_1.0 | reduce | flops 2838528 | bytes 9461762 | tf_op jit(solution)/shard_map/reduce_sum | solution.py:74
  135.9 0.6 copy.17
  (5 shorter events, 0.0 us)
Async XLA Ops:
  0.6 21.0 %copy-start = (bf16[1,1024,924]{1,2,0:T(8,128)(2,1)S(1)}, bf16[1,1024,924]{1,2,0:T(8,128)(2,1)}, u32[]{:S(2)}) copy-start(bf16[1,1024,924]{1,2,0:T(8,128)(2,1)} %param.9) | copy-start | bytes 5677060
  23.0 17.3 %copy-start.1 = (bf16[1,1,8,4096]{3,2,1,0:T(8,128)(2,1)S(1)}, bf16[1,1,8,4096]{3,2,1,0:T(8,128)(2,1)}, u32[]{:S(2)}) copy-start(bf16[1,1,8,4096]{3,2,1,0:T(8,128)(2,1)} %param.5) | copy-start | bytes 196612
  41.3 32.5 %all-to-all-start.3 = ((bf16[16,8,4096]{2,1,0:T(8,128)(2,1)}), bf16[16,8,4096]{2,1,0:T(8,128)(2,1)}, u32[]{:S(2)}, u32[]{:S(2)}) async-start(bf16[16,8,4096]{2,1,0:T(8,128)(2,1)} %broadcast_in_dim.14), calls=%async_computation.3 | async-start | bytes 2097152 | tf_op jit(solution)/shard_map/all_to_all | solution.py:20
  73.8 30.3 %all-to-all-start.2 = ((bf16[16,8,4096]{2,1,0:T(8,128)(2,1)}), bf16[16,8,4096]{2,1,0:T(8,128)(2,1)}, u32[]{:S(2)}, u32[]{:S(2)}) async-start(bf16[16,8,4096]{2,1,0:T(8,128)(2,1)} %reshape.27), calls=%async_computation.2 | async-start | bytes 2097152 | tf_op jit(solution)/shard_map/all_to_all | solution.py:14
  104.1 18.6 %all-to-all-start.4 = ((bf16[128,4,1024]{2,0,1:T(8,128)(2,1)}), bf16[128,4,1024]{2,0,1:T(8,128)(2,1)}, u32[]{:S(2)}, u32[]{:S(2)}) async-start(bf16[128,4,1024]{2,0,1:T(8,128)(2,1)} %copy.12), calls=%async_computation.4 | async-start | bytes 2097152 | tf_op jit(solution)/shard_map/all_to_all | solution.py:66
  109.7 26.2 %collective-permute-start = (bf16[8,4096]{1,0:T(8,128)(2,1)S(1)}, bf16[8,4096]{1,0:T(8,128)(2,1)S(1)}, u32[]{:S(2)}, u32[]{:S(2)}) collective-permute-start(bf16[8,4096]{1,0:T(8,128)(2,1)S(1)} %reduce_sum.24), channel_id=1, source_target_pairs={{64,0},{128,64},{192,128},{65,1},{129,65},{193,129},{66,2},{130,66... | collective-permute-start | bytes 196616 | tf_op jit(solution)/shard_map/ppermute | solution.py:37
where the time goes:
time: 137 us
  waiting for transfers between devices  49 us (36%)
  blocking collectives  35.5 us (26%)
  starting transfers between devices  20.1 us (15%)
  local copies, waits for them, and re-layouts  13.7 us (10%)
  other arithmetic  9.78 us (7%)
  matrix products  7.67 us (6%)
    all_to_all x1, waiting for transfers between devices, sent_and_summed(): lax.all_to_all(tiles, axis, split_axis=0, concat_axis=0, tiled=True)  19.1 us
    all_to_all x1, blocking collectives, from_everyone(): return lax.all_to_all(copies, axis, split_axis=0, concat_axis=0, tiled=True)  18.3 us
    all_to_all x1, waiting for transfers between devices, from_everyone(): return lax.all_to_all(copies, axis, split_axis=0, concat_axis=0, tiled=True)  18.3 us
    all_to_all x1, blocking collectives, on_device(): lax.all_to_all(partial_value.astype(jnp.bfloat16), 'dp', split_axis=0, co...  17.2 us
    all_to_all x1, waiting for transfers between devices, on_device(): lax.all_to_all(gathered_in, 'dp', split_axis=1, concat_axis=0, tiled=True)  11.7 us
    all_to_all x1, starting transfers between devices, from_everyone(): return lax.all_to_all(copies, axis, split_axis=0, concat_axis=0, tiled=True)  8.6 us
    reduce_sum x1, other arithmetic, on_device(): grads_total = jnp.sum(rounded.astype(jnp.float32), axis=0)  6.88 us
    dot_general x1, matrix products, on_device(): lax.dot_general(in_columns.reshape(groups, rows_total, in_columns.shape[1...  6.38 us
  transfers between devices with their start and end apart: 4, of which 3 were waited for; matrix products, arithmetic and copies ran while one was open for 17% of the time, Pallas kernels for 0%

commit v1 on v0

--- a/solution.py
+++ b/solution.py
@@ -2,6 +2,29 @@
 import jax.numpy as jnp
 from jax import lax
 from jax.sharding import PartitionSpec as P
+
+
+def split_up(x, dim, count):
+    shape = x.shape
+    blocks = x.reshape(*shape[:dim], count, shape[dim] // count, *shape[dim + 1 :])
+    return jnp.moveaxis(blocks, dim, 0)
+
+
+def joined_along(blocks, dim):
+    blocks = jnp.moveaxis(blocks, 0, dim)
+    shape = blocks.shape
+    return blocks.reshape(*shape[:dim], shape[dim] * shape[dim + 1], *shape[dim + 2 :])
+
+
+def exchange_directly(x, axis, split_dim, concat_dim):
+    length, place = (lax.axis_size(axis), lax.axis_index(axis))
+    blocks = split_up(x, split_dim, length)
+    done = [blocks[place]]
+    for step in range(1, length):
+        sent = blocks[(place + step) % length]
+        done.append(lax.ppermute(sent, axis, [(i, (i + step) % length) for i in range(length)]))
+    blocks = jnp.stack(done)[(place - jnp.arange(length)) % length]
+    return joined_along(blocks, concat_dim)
 
 
 def cut_along(x, dim, peers):
@@ -59,9 +82,9 @@
     partial_value = lax.dot_general(
         all_grads, gate_local, contract_cols, preferred_element_type=jnp.float32
     )
-    returned = lax.all_to_all(
-        partial_value.astype(jnp.bfloat16), "dp", split_axis=0, concat_axis=1, tiled=True
-    ).astype(partial_value.dtype)
+    returned = exchange_directly(partial_value.astype(jnp.bfloat16), "dp", 0, 1).astype(
+        partial_value.dtype
+    )
     input_grad = finish(returned)
     in_columns = lax.all_to_all(gathered_in, "dp", split_axis=1, concat_axis=0, tiled=True)
     products = lax.dot_general(

time: 137 us -> 125 us (0.912)
  blocking collectives: 35.5 us -> 18.3 us
  starting transfers between devices: 20.1 us -> 25.1 us
  waiting for transfers between devices: 49 us -> 44.7 us
  local copies, waits for them, and re-layouts: 13.7 us -> 16.6 us
    all_to_all x1, waiting for transfers between devices: 18.3 us -> 0.01 us  [from_everyone(): return lax.all_to_all(copies, axis, split_axis=0, concat_axis=0, tiled=True)]
    all_to_all x1 -> x0, blocking collectives: 17.2 us -> none  [on_device(): lax.all_to_all(partial_value.astype(jnp.bfloat16), 'dp', split_axis=0, co...]
    ppermute x0 -> x3, waiting for transfers between devices: none -> 11.4 us  [exchange_directly(): lax.ppermute(sent, axis, [(i, (i + step) % length) for i in range(length)])]
    all_to_all x1 -> x0, local copies, waits for them, and re-layouts: 3 us -> none  [on_device(): lax.all_to_all(partial_value.astype(jnp.bfloat16), 'dp', split_axis=0, co...]
    transpose x0 -> x1, local copies, waits for them, and re-layouts: none -> 3 us  [joined_along(): blocks = jnp.moveaxis(blocks, 0, dim)]
    gather x0 -> x1, local copies, waits for them, and re-layouts: none -> 2.82 us  [exchange_directly(): blocks = jnp.stack(done)[(place - jnp.arange(length)) % length]]
    ppermute x0 -> x3, starting transfers between devices: none -> 2.71 us  [exchange_directly(): lax.ppermute(sent, axis, [(i, (i + step) % length) for i in range(length)])]
    all_to_all x1, starting transfers between devices: 5.99 us -> 8.13 us  [sent_and_summed(): lax.all_to_all(tiles, axis, split_axis=0, concat_axis=0, tiled=True)]
  transfers between devices with their start and end apart: 4 -> 7, of which waited for: 3 -> 5; matrix products, arithmetic and copies ran while one was open for 17% -> 23% of each run, Pallas kernels for 0% -> 0%
where the time goes in v1:
time: 125 us; the launch traced here: 124 us
  waiting for transfers between devices  44.7 us (36%)
  starting transfers between devices  25.1 us (20%)
  blocking collectives  18.3 us (15%)
  local copies, waits for them, and re-layouts  16.6 us (13%)
  other arithmetic  10.9 us (9%)
  matrix products  7.67 us (6%)
    all_to_all x1, waiting for transfers between devices, sent_and_summed(): lax.all_to_all(tiles, axis, split_axis=0, concat_axis=0, tiled=True)  20.5 us
    all_to_all x1, blocking collectives, from_everyone(): return lax.all_to_all(copies, axis, split_axis=0, concat_axis=0, tiled=True)  18.3 us
    all_to_all x1, waiting for transfers between devices, on_device(): lax.all_to_all(gathered_in, 'dp', split_axis=1, concat_axis=0, tiled=True)  12.8 us
    ppermute x3, waiting for transfers between devices, exchange_directly(): lax.ppermute(sent, axis, [(i, (i + step) % length) for i in range(length)])  11.4 us
    all_to_all x1, starting transfers between devices, from_everyone(): return lax.all_to_all(copies, axis, split_axis=0, concat_axis=0, tiled=True)  8.61 us
    all_to_all x1, starting transfers between devices, sent_and_summed(): lax.all_to_all(tiles, axis, split_axis=0, concat_axis=0, tiled=True)  8.13 us
    reduce_sum x1, other arithmetic, on_device(): grads_total = jnp.sum(rounded.astype(jnp.float32), axis=0)  6.88 us
    dot_general x1, matrix products, on_device(): lax.dot_general(in_columns.reshape(groups, rows_total, in_columns.shape[1...  6.37 us
  transfers between devices with their start and end apart: 7, of which 5 were waited for; matrix products, arithmetic and copies ran while one was open for 23% of the time, Pallas kernels for 0%

profile of v1, /device:TPU:96, one launch (start us, length us, event | category | flops | bytes accessed | tf_op | source)
XLA Modules:
  0.0 124.1 jit_solution(1561047385991948686)
XLA Ops:
  0.7 1.5 %fusion.11 = bf16[128,924]{0,1:T(8,128)(2,1)S(1)} fusion(bf16[1,1,128,924]{2,3,1,0:T(8,128)(2,1)} %param.7, bf16[1,1,128,924]{2,3,1,0:T(8,128)(2,1)} %param.8, bf16[1,1,128,924]{2,3,1,0:T(8,128)(2,1)} %param.6), kind=kLoop, calls=%fused_computation.15 | loop fusion | flops 1537536 | bytes 946176 | tf_op jit(solution)/shard_map/convert_element_type | solution.py:76
  2.3 18.3 %all_to_all.31 = bf16[4,128,924]{1,2,0:T(8,128)(2,1)S(1)} all-to-all(bf16[4,128,924]{1,2,0:T(8,128)(2,1)S(1)} %broadcast_in_dim.13), channel_id=1, replica_groups=mesh['pp'=4,'tp'=16,'dp'=4] {'dp'}, dimensions={0} | all-to-all | bytes 1892352 | tf_op jit(solution)/shard_map/all_to_all | solution.py:43
  20.6 1.1 broadcast_in_dim.15
  21.8 8.6 %all-to-all-start.2 = ((bf16[16,8,4096]{2,1,0:T(8,128)(2,1)}), bf16[16,8,4096]{2,1,0:T(8,128)(2,1)}, u32[]{:S(2)}, u32[]{:S(2)}) async-start(bf16[16,8,4096]{2,1,0:T(8,128)(2,1)} %broadcast_in_dim.15), calls=%async_computation.2 | async-start | bytes 2097152 | tf_op jit(solution)/shard_map/all_to_all | solution.py:43
  31.4 1.3 %fusion.2 = bf16[512,1024]{1,0:T(8,128)(2,1)S(1)} fusion(bf16[512,924]{0,1:T(8,128)(2,1)S(1)} %bitcast.47, bf16[1,1024,924]{1,2,0:T(8,128)(2,1)S(1)} %copy-done), kind=kOutput, calls=%fused_computation.4 | convolution fusion | flops 969408512 | bytes 3887104 | tf_op jit(solution)/shard_map/dot_general | solution.py:82
  32.8 1.2 %collective-permute-start.2 = (bf16[128,1024]{1,0:T(8,128)(2,1)S(1)}, bf16[128,1024]{1,0:T(8,128)(2,1)S(1)}, u32[]{:S(2)}, u32[]{:S(2)}) collective-permute-start(bf16[128,1024]{1,0:T(8,128)(2,1)S(1)} %get-tuple-element.3), channel_id=1, source_target_pairs={{0,3},{1,0},{2,1},{3,2},{4,7},{5,4},{6,5},{7,6},{8,11},{9,8},{10,9... | collective-permute-start | bytes 786440 | tf_op jit(solution)/shard_map/ppermute | solution.py:25
  34.1 1.5 %collective-permute-start.1 = (bf16[128,1024]{1,0:T(8,128)(2,1)S(1)}, bf16[128,1024]{1,0:T(8,128)(2,1)S(1)}, u32[]{:S(2)}, u32[]{:S(2)}) collective-permute-start(bf16[128,1024]{1,0:T(8,128)(2,1)S(1)} %get-tuple-element.4), channel_id=1, source_target_pairs={{0,2},{1,3},{2,0},{3,1},{4,6},{5,7},{6,4},{7,5},{8,10},{9,11},{10,... | collective-permute-start | bytes 786440 | tf_op jit(solution)/shard_map/ppermute | solution.py:25
  35.6 6.2 %collective-permute-done.2 = bf16[128,1024]{1,0:T(8,128)(2,1)S(1)} collective-permute-done((bf16[128,1024]{1,0:T(8,128)(2,1)S(1)}, bf16[128,1024]{1,0:T(8,128)(2,1)S(1)}, u32[]{:S(2)}, u32[]{:S(2)}) %collective-permute-start.2) | collective-permute-done | bytes 262176 | tf_op jit(solution)/shard_map/ppermute | solution.py:25
  41.8 2.4 %collective-permute-done.1 = bf16[128,1024]{1,0:T(8,128)(2,1)S(1)} collective-permute-done((bf16[128,1024]{1,0:T(8,128)(2,1)S(1)}, bf16[128,1024]{1,0:T(8,128)(2,1)S(1)}, u32[]{:S(2)}, u32[]{:S(2)}) %collective-permute-start.1) | collective-permute-done | bytes 262176 | tf_op jit(solution)/shard_map/ppermute | solution.py:25
  44.2 2.8 %collective-permute-done = bf16[128,1024]{1,0:T(8,128)(2,1)S(1)} collective-permute-done((bf16[128,1024]{1,0:T(8,128)(2,1)S(1)}, bf16[128,1024]{1,0:T(8,128)(2,1)S(1)}, u32[]{:S(2)}, u32[]{:S(2)}) %collective-permute-start) | collective-permute-done | bytes 262176 | tf_op jit(solution)/shard_map/ppermute | solution.py:25
  47.0 1.1 pad_maximum_fusion
  48.1 2.8 %gather_fusion = bf16[4,128,1024]{2,1,0:T(8,128)(2,1)} fusion(bf16[4,128,1024]{2,1,0:T(8,128)(2,1)} %pad_maximum_fusion, s32[1024]{0:T(1024)S(1)} %pad_clamp_fusion), kind=kCustom, calls=%fused_computation | custom fusion | bytes 2097168 | tf_op jit(solution)/shard_map/gather | solution.py:26
  50.9 3.0 %copy.10 = bf16[128,4,1024]{2,1,0:T(4,128)(2,1)} copy(bf16[128,4,1024]{2,0,1:T(8,128)(2,1)} %bitcast.42) | data formatting | bytes 2097152 | tf_op jit(solution)/shard_map/transpose | solution.py:14
  53.9 2.6 %reshape.78 = bf16[16,8,4096]{2,1,0:T(8,128)(2,1)} reshape(bf16[128,4,1024]{2,1,0:T(4,128)(2,1)} %copy.10) | data formatting | bytes 2097152 | tf_op jit(solution)/shard_map/reshape | solution.py:32
  56.5 8.1 %all-to-all-start.1 = ((bf16[16,8,4096]{2,1,0:T(8,128)(2,1)}), bf16[16,8,4096]{2,1,0:T(8,128)(2,1)}, u32[]{:S(2)}, u32[]{:S(2)}) async-start(bf16[16,8,4096]{2,1,0:T(8,128)(2,1)} %reshape.78), calls=%async_computation.1 | async-start | bytes 2097152 | tf_op jit(solution)/shard_map/all_to_all | solution.py:37
  64.6 2.6 %all_to_all.24 = bf16[128,4,1024]{2,1,0:T(4,128)(2,1)} reshape(bf16[16,8,4096]{2,1,0:T(8,128)(2,1)} %all-to-all-done.2) | data formatting | bytes 2097152 | tf_op jit(solution)/shard_map/all_to_all | solution.py:89
  67.3 2.5 %copy.11 = bf16[128,4,1024]{2,0,1:T(8,128)(2,1)} copy(bf16[128,4,1024]{2,1,0:T(4,128)(2,1)} %all_to_all.24) | data formatting | bytes 2097152 | tf_op jit(solution)/shard_map/all_to_all | solution.py:89
  69.8 20.5 %all-to-all-done.1 = bf16[16,8,4096]{2,1,0:T(8,128)(2,1)} async-done(((bf16[16,8,4096]{2,1,0:T(8,128)(2,1)}), bf16[16,8,4096]{2,1,0:T(8,128)(2,1)}, u32[]{:S(2)}, u32[]{:S(2)}) %all-to-all-start.1) | async-done | bytes 1048608 | tf_op jit(solution)/shard_map/all_to_all | solution.py:37
  90.3 4.2 %all-to-all-start.3 = ((bf16[128,4,1024]{2,0,1:T(8,128)(2,1)}), bf16[128,4,1024]{2,0,1:T(8,128)(2,1)}, u32[]{:S(2)}, u32[]{:S(2)}) async-start(bf16[128,4,1024]{2,0,1:T(8,128)(2,1)} %copy.11), calls=%async_computation.3 | async-start | bytes 2097152 | tf_op jit(solution)/shard_map/all_to_all | solution.py:89
  94.6 1.4 %reduce_sum.24 = bf16[8,4096]{1,0:T(8,128)(2,1)S(1)} reduce(bf16[16,8,4096]{2,1,0:T(8,128)(2,1)} %all-to-all-done.1, bf16[]{:T(256)} %constant.46.clone.1), dimensions={0}, to_apply=%region_0.1 | reduce | flops 491520 | bytes 1114114 | tf_op jit(solution)/shard_map/reduce_sum | solution.py:38
  95.9 1.5 %collective-permute-start.3 = (bf16[8,4096]{1,0:T(8,128)(2,1)S(1)}, bf16[8,4096]{1,0:T(8,128)(2,1)S(1)}, u32[]{:S(2)}, u32[]{:S(2)}) collective-permute-start(bf16[8,4096]{1,0:T(8,128)(2,1)S(1)} %reduce_sum.24), channel_id=1, source_target_pairs={{64,0},{128,64},{192,128},{65,1},{129,65},{193,129},{66,2},{130,66... | collective-permute-start | bytes 196616 | tf_op jit(solution)/shard_map/ppermute | solution.py:60
  97.4 12.8 %all-to-all-done.3 = bf16[128,4,1024]{2,0,1:T(8,128)(2,1)} async-done(((bf16[128,4,1024]{2,0,1:T(8,128)(2,1)}), bf16[128,4,1024]{2,0,1:T(8,128)(2,1)}, u32[]{:S(2)}, u32[]{:S(2)}) %all-to-all-start.3) | async-done | bytes 1048608 | tf_op jit(solution)/shard_map/all_to_all | solution.py:89
  110.2 6.4 %convert_bitcast_fusion = bf16[4,1024,924]{1,2,0:T(8,128)(2,1)} fusion(bf16[4,128,924]{1,2,0:T(8,128)(2,1)S(1)} %all_to_all.31, bf16[128,4,1024]{2,0,1:T(8,128)(2,1)} %all-to-all-done.3), kind=kOutput, calls=%fused_computation.1 | convolution fusion | flops 972668928 | bytes 9564160 | tf_op jit(solution)/shard_map/dot_general | solution.py:90
  116.5 6.9 %reduce_sum.25 = bf16[1024,924]{0,1:T(8,128)(2,1)} reduce(bf16[4,1024,924]{1,2,0:T(8,128)(2,1)} %convert_bitcast_fusion, bf16[]{:T(256)} %constant.46.clone.1), dimensions={0}, to_apply=%region_1.2 | reduce | flops 2838528 | bytes 9461762 | tf_op jit(solution)/shard_map/reduce_sum | solution.py:97
  (15 shorter events, 1.9 us)
Async XLA Ops:
  0.6 30.8 %copy-start = (bf16[1,1024,924]{1,2,0:T(8,128)(2,1)S(1)}, bf16[1,1024,924]{1,2,0:T(8,128)(2,1)}, u32[]{:S(2)}) copy-start(bf16[1,1024,924]{1,2,0:T(8,128)(2,1)} %param.9) | copy-start | bytes 5677060
  0.6 20.0 %copy-start.1 = (bf16[1,1,8,4096]{3,2,1,0:T(8,128)(2,1)S(1)}, bf16[1,1,8,4096]{3,2,1,0:T(8,128)(2,1)}, u32[]{:S(2)}) copy-start(bf16[1,1,8,4096]{3,2,1,0:T(8,128)(2,1)} %param.5) | copy-start | bytes 196612
  21.8 34.7 %all-to-all-start.2 = ((bf16[16,8,4096]{2,1,0:T(8,128)(2,1)}), bf16[16,8,4096]{2,1,0:T(8,128)(2,1)}, u32[]{:S(2)}, u32[]{:S(2)}) async-start(bf16[16,8,4096]{2,1,0:T(8,128)(2,1)} %broadcast_in_dim.15), calls=%async_computation.2 | async-start | bytes 2097152 | tf_op jit(solution)/shard_map/all_to_all | solution.py:43
  32.8 8.9 %collective-permute-start.2 = (bf16[128,1024]{1,0:T(8,128)(2,1)S(1)}, bf16[128,1024]{1,0:T(8,128)(2,1)S(1)}, u32[]{:S(2)}, u32[]{:S(2)}) collective-permute-start(bf16[128,1024]{1,0:T(8,128)(2,1)S(1)} %get-tuple-element.3), channel_id=1, source_target_pairs={{0,3},{1,0},{2,1},{3,2},{4,7},{5,4},{6,5},{7,6},{8,11},{9,8},{10,9... | collective-permute-start | bytes 786440 | tf_op jit(solution)/shard_map/ppermute | solution.py:25
  34.1 10.1 %collective-permute-start.1 = (bf16[128,1024]{1,0:T(8,128)(2,1)S(1)}, bf16[128,1024]{1,0:T(8,128)(2,1)S(1)}, u32[]{:S(2)}, u32[]{:S(2)}) collective-permute-start(bf16[128,1024]{1,0:T(8,128)(2,1)S(1)} %get-tuple-element.4), channel_id=1, source_target_pairs={{0,2},{1,3},{2,0},{3,1},{4,6},{5,7},{6,4},{7,5},{8,10},{9,11},{10,... | collective-permute-start | bytes 786440 | tf_op jit(solution)/shard_map/ppermute | solution.py:25
  35.5 11.4 %collective-permute-start = (bf16[128,1024]{1,0:T(8,128)(2,1)S(1)}, bf16[128,1024]{1,0:T(8,128)(2,1)S(1)}, u32[]{:S(2)}, u32[]{:S(2)}) collective-permute-start(bf16[128,1024]{1,0:T(8,128)(2,1)S(1)} %get-tuple-element.5), channel_id=1, source_target_pairs={{0,1},{1,2},{2,3},{3,0},{4,5},{5,6},{6,7},{7,4},{8,9},{9,10},{10,1... | collective-permute-start | bytes 786440 | tf_op jit(solution)/shard_map/ppermute | solution.py:25
  56.5 33.8 %all-to-all-start.1 = ((bf16[16,8,4096]{2,1,0:T(8,128)(2,1)}), bf16[16,8,4096]{2,1,0:T(8,128)(2,1)}, u32[]{:S(2)}, u32[]{:S(2)}) async-start(bf16[16,8,4096]{2,1,0:T(8,128)(2,1)} %reshape.78), calls=%async_computation.1 | async-start | bytes 2097152 | tf_op jit(solution)/shard_map/all_to_all | solution.py:37
  90.3 19.8 %all-to-all-start.3 = ((bf16[128,4,1024]{2,0,1:T(8,128)(2,1)}), bf16[128,4,1024]{2,0,1:T(8,128)(2,1)}, u32[]{:S(2)}, u32[]{:S(2)}) async-start(bf16[128,4,1024]{2,0,1:T(8,128)(2,1)} %copy.11), calls=%async_computation.3 | async-start | bytes 2097152 | tf_op jit(solution)/shard_map/all_to_all | solution.py:89
  95.9 27.5 %collective-permute-start.3 = (bf16[8,4096]{1,0:T(8,128)(2,1)S(1)}, bf16[8,4096]{1,0:T(8,128)(2,1)S(1)}, u32[]{:S(2)}, u32[]{:S(2)}) collective-permute-start(bf16[8,4096]{1,0:T(8,128)(2,1)S(1)} %reduce_sum.24), channel_id=1, source_target_pairs={{64,0},{128,64},{192,128},{65,1},{129,65},{193,129},{66,2},{130,66... | collective-permute-start | bytes 196616 | tf_op jit(solution)/shard_map/ppermute | solution.py:60
